TPU v7x, 32 devices: a whole 2x2x4 slice. The times are simulated.
32 devices in a mesh: dp: 8 (over y, x, core), expert: 4 (over z).
Axes of the slice: x: 2, y: 2, z: 4, core: 2. Of those that a mesh axis runs over, the one named last changes fastest.
Arguments:
- tokens_in: bfloat16 [4096, 2048], P(('dp', 'expert')), may hold values from -6 to 6
- out_grad: bfloat16 [4096, 2048], P(('dp', 'expert')), may hold values from -3 to 3
- expert_ids: int32 [4096, 8], P(('dp', 'expert')), may hold values from 0 to 127, all different within a row; in each aligned block of 128 rows (0 to 127, 128 to 255, ...) at most 16 rows name the same one
- rest_scores: float32 [4096, 8], P(('dp', 'expert')), may hold values from -60 to 60
- router_weight: bfloat16 [2048, 128], replicated, may hold values from -0.125 to 0.125
- down_weight: bfloat16 [4, 768, 2048], P('expert'), may hold values from -0.125 to 0.125
- saved_hidden: bfloat16 [8, 4, 4, 16, 768], P('dp', 'expert'), may hold values from -6 to 6
Outputs:
- token_grad: bfloat16 [4096, 2048], P(('dp', 'expert'))
- router_grad: float32 [2048, 128], P('dp', 'expert')
- down_grad: float32 [4, 768, 2048], P('expert', 'dp')
- hidden_grad: bfloat16 [8, 4, 4, 16, 768], P('dp', 'expert')
Inputs may be any that keep to these rules, and one draw needn't show every extreme that they name: `expert_ids`: each row names 8 different experts; among the 128 tokens of one device no expert is named more than 16 times, a bound that some block reaches.
All inputs are finite; a program needn't handle non-finite values.
Results may differ from a plain program's by a relative error of at most 0.024.
Values may be sent and summed in bfloat16 or wider, within the bound.
A program may use at most 64 MiB of HBM per device.

v0:
```python
import functools
import jax
import jax.numpy as jnp
from jax import lax
from jax.experimental import pallas as pl
from jax.experimental.pallas import tpu as pltpu
from jax.sharding import PartitionSpec as P


def slot_layout(ids_block, window, capacity):
    hit_mask = (ids_block[:, :, None] == jnp.arange(window, dtype=jnp.int32)[None, None, :]).astype(
        jnp.int32
    )
    chosen = jnp.sum(hit_mask, axis=1)
    before = jnp.cumsum(chosen, axis=0) - chosen
    placed = (chosen[None, :, :] == 1) & (
        before[None, :, :] == jnp.arange(capacity, dtype=jnp.int32)[:, None, None]
    )
    slot_table = jnp.transpose(placed, (2, 0, 1)).astype(jnp.float32)
    return (slot_table, hit_mask.astype(jnp.float32))


def shards(tokens_in, out_grad, expert_ids, rest_scores, router_weight, down_weight, saved_hidden):
    window = lax.axis_size("expert")
    capacity = saved_hidden.shape[3]
    sources = saved_hidden.shape[2]
    hidden_units = saved_hidden.shape[4]
    width = out_grad.shape[1]
    scored = router_weight.shape[1]
    logits = jnp.dot(tokens_in, router_weight, preferred_element_type=jnp.float32)
    all_mask = (
        expert_ids[:, :, None] == jnp.arange(scored, dtype=jnp.int32)[None, None, :]
    ).astype(jnp.float32)
    picked = jnp.sum(all_mask * logits[:, None, :], axis=2)
    gate_sel = jax.nn.softmax(picked, axis=1)
    slot_table, hit_mask = slot_layout(expert_ids, window, capacity)
    gate_each = jnp.einsum("tkw,tk->tw", hit_mask, gate_sel)
    sent_grad = jnp.einsum(
        "wct,td->wcd", slot_table.astype(jnp.bfloat16), out_grad, preferred_element_type=jnp.float32
    ).astype(jnp.bfloat16)
    sent_gate = jnp.einsum("wct,tw->wc", slot_table, gate_each).astype(jnp.bfloat16)
    got_grad, got_gate = (
        lax.all_to_all(sent_grad, "expert", split_axis=0, concat_axis=0, tiled=True),
        lax.all_to_all(sent_gate, "expert", split_axis=0, concat_axis=0, tiled=True),
    )
    slot_rows = got_grad.reshape(sources * capacity, width)
    gate_flat = got_gate.reshape(sources * capacity).astype(jnp.float32)
    weight_now = down_weight[0]
    raw_grad = lax.dot_general(
        slot_rows, weight_now, (((1,), (1,)), ((), ())), preferred_element_type=jnp.float32
    )
    hidden_flat = saved_hidden[0, 0].reshape(sources * capacity, hidden_units)
    hid_grad = (gate_flat[:, None] * raw_grad).astype(jnp.bfloat16)
    scores = jnp.sum(raw_grad * hidden_flat.astype(jnp.float32), axis=1).reshape(sources, capacity)
    scaled = (gate_flat[:, None] * slot_rows.astype(jnp.float32)).astype(jnp.bfloat16)
    down_grad = lax.psum_scatter(
        lax.dot_general(
            hidden_flat, scaled, (((0,), (0,)), ((), ())), preferred_element_type=jnp.float32
        ).astype(jnp.bfloat16),
        "dp",
        scatter_dimension=0,
        tiled=True,
    ).astype(jnp.float32)
    returned = lax.all_to_all(scores, "expert", split_axis=0, concat_axis=0, tiled=True)
    per_token = jnp.einsum("wct,wc->tw", slot_table, returned)
    score_tok = jnp.einsum("tkw,tw->tk", hit_mask, per_token)
    score_all = jnp.where(expert_ids < window, score_tok, rest_scores)
    mean_part = jnp.sum(gate_sel * score_all, axis=1, keepdims=True)
    logit_sel = gate_sel * (score_all - mean_part)
    logit_bf = jnp.einsum("tke,tk->te", all_mask, logit_sel).astype(jnp.bfloat16)
    summed_rows = lax.psum_scatter(
        lax.dot_general(
            tokens_in, logit_bf, (((0,), (0,)), ((), ())), preferred_element_type=jnp.float32
        ).astype(jnp.bfloat16),
        "dp",
        scatter_dimension=0,
        tiled=True,
    )
    router_grad = lax.psum_scatter(summed_rows, "expert", scatter_dimension=1, tiled=True).astype(
        jnp.float32
    )
    token_grad = lax.dot_general(
        logit_bf, router_weight, (((1,), (1,)), ((), ())), preferred_element_type=jnp.float32
    ).astype(jnp.bfloat16)
    hidden_grad = hid_grad.reshape(1, 1, sources, capacity, hidden_units)
    return (token_grad, router_grad, down_grad[None], hidden_grad)


MESH = pl.DeviceIdType.MESH
F32, BF16 = jnp.float32, jnp.bfloat16


def flip(index, mask):
    out = 0
    for bit in (1, 2, 4):
        digit = lax.rem(lax.div(index, bit), 2)
        out = out + bit * ((1 - digit) if mask & bit else digit)
    return out


def rows_times(a, b):
    return lax.dot_general(a, b, (((1,), (1,)), ((), ())), preferred_element_type=F32)


def times(a, b):
    return lax.dot_general(a, b, (((1,), (0,)), ((), ())), preferred_element_type=F32)


def layer_kernel(
    nd, nz, cap,
    tok_h, grad_h, ids_h, rest_h, rw_h, w_h, hid_h,
    token_o, router_o, down_o, hidden_o,
    tok, grad, ids, rest, rw, weight, hid,
    blk, gat, y, gate_s, gate_r, ret_s, ret_r, tok_all, lt, lt_all, hg_s, hg_all, rg_s, rg_r,
    token_v, router_v, down_v, hidden_v,
    load_sem, store_sem, disp_s, disp_r, gsem_s, gsem_r, ag_s, ag_r, tk_s, tk_r,
    rs_s, rs_r, lg_s, lg_r, hs_s, hs_r, zr_s, zr_r,
):
    me = lax.axis_index("dp")
    mz = lax.axis_index("expert")
    tokens, width = tok.shape
    experts = rw.shape[1]
    slots = nz * cap
    hidden_units = hid.shape[1]
    own_cols = width // nd

    loads = []
    for i, (src, dst) in enumerate(
        ((ids_h, ids), (grad_h, grad), (tok_h, tok), (rw_h, rw), (rest_h, rest), (hid_h, hid), (w_h, weight))
    ):
        loads.append(pltpu.make_async_copy(src, dst, load_sem.at[i]))
        loads[-1].start()
    ld_ids, ld_grad, ld_tok, ld_rw, ld_rest, ld_hid, ld_w = loads

    peers = [flip(me, p) for p in range(nd)]
    half = lax.div(mz, 2)
    near = [mz, mz + 1 - 2 * lax.rem(mz, 2), 2 - half, 3 - 3 * half]
    barrier = pltpu.get_barrier_semaphore()
    for p in range(1, nd):
        pl.semaphore_signal(barrier, inc=1, device_id=(peers[p], mz), device_id_type=MESH)
    for k in range(1, nz):
        pl.semaphore_signal(barrier, inc=1, device_id=(me, near[k]), device_id_type=MESH)

    sent = []

    def send(src, dst, s_sem, r_sem, device):
        copy = pltpu.make_async_remote_copy(
            src_ref=src, dst_ref=dst, send_sem=s_sem, recv_sem=r_sem, device_id=device, device_id_type=MESH
        )
        copy.start()
        sent.append(copy)

    def arrived(ref, r_sem):
        pltpu.make_async_copy(ref, ref, r_sem).wait()

    e_row = lax.broadcasted_iota(jnp.int32, (experts, tokens), 0)
    ld_ids.wait()
    idv = ids[...]
    topk = idv.shape[0]
    hits = [idv[k : k + 1, :] == e_row for k in range(topk)]
    mask = hits[0]
    for k in range(1, topk):
        mask = mask | hits[k]
    t_row = lax.broadcasted_iota(jnp.int32, (tokens, tokens), 0)
    t_col = lax.broadcasted_iota(jnp.int32, (tokens, tokens), 1)
    earlier = jnp.where(t_row < t_col, 1.0, 0.0).astype(BF16)
    chosen = jnp.where(mask, 1.0, 0.0)
    place = jnp.where(mask, times(chosen.astype(BF16), earlier), -1.0)
    c_row = lax.broadcasted_iota(jnp.int32, (cap, tokens), 0).astype(F32)
    tables = [jnp.where(place[e : e + 1, :] == c_row, 1.0, 0.0) for e in range(nz)]
    table = jnp.concatenate(tables, axis=0).astype(BF16)

    ld_grad.wait()
    for e in range(nz):
        blk[e] = times(table[e * cap : (e + 1) * cap], grad[...]).astype(BF16)
    gat[me, mz] = blk[mz]

    pl.semaphore_wait(barrier, nd - 1 + nz - 1)
    for k in Z_ORDER:
        send(blk.at[near[k]], gat.at[me, mz], disp_s.at[k], disp_r.at[mz], (me, near[k]))

    def spread(ref, k, origin, target, n):
        send(ref, ref, ag_s.at[k, n], ag_r.at[k, origin ^ target], (peers[target], mz))

    def landed(k):
        arrived(gat.at[me, near[k]], disp_r.at[near[k]])

    def spread_own(k):
        ref = gat.at[me, near[k]]
        for n, target in enumerate((2, 4, 1)):
            spread(ref, k, 0, target, n)

    def relay_near(k):
        via = 2 if k % 2 == 0 else 4
        for origin in (via, 6 - via):
            ref = gat.at[peers[origin], near[k]]
            arrived(ref, ag_r.at[k, origin])
            if origin == via:
                spread(ref, k, origin, 6 - via, 3)
            spread(ref, k, origin, 1, 4 + (origin // 4))

    def relay_far(k):
        ref = gat.at[peers[6], near[k]]
        arrived(ref, ag_r.at[k, 6])
        spread(ref, k, 6, 1, 6)

    spread_own(0)

    ld_tok.wait()
    for p in TOKEN_ORDER:
        cols = pl.ds(pl.multiple_of(peers[p] * own_cols, own_cols), own_cols)
        send(tok.at[:, cols], tok_all.at[me], tk_s.at[p], tk_r.at[p], (peers[p], mz))


    ld_rw.wait()
    logits = times(tok[...], rw[...]).T
    low = jnp.where(mask, logits, -3.0e38)
    raised = jnp.where(mask, jnp.exp(low - jnp.max(low, axis=0, keepdims=True)), 0.0)
    gate = raised / jnp.sum(raised, axis=0, keepdims=True)
    for e in range(nz):
        one = jnp.sum(tables[e] * gate[e : e + 1, :], axis=1, keepdims=True)
        gate_s[e] = jnp.broadcast_to(one, (cap, experts)).astype(BF16)
    gate_r[mz] = gate_s[mz]
    for k in range(1, nz):
        send(gate_s.at[near[k]], gate_r.at[mz], gsem_s.at[k], gsem_r.at[mz], (me, near[k]))

    ld_hid.wait()
    ld_w.wait()
    y[...] = times(hid[...], weight[...]).reshape(y.shape)

    ld_rest.wait()
    restv = rest[...]
    rest_all = jnp.where(hits[0], restv[0:1, :], 0.0)
    for k in range(1, topk):
        rest_all = rest_all + jnp.where(hits[k], restv[k : k + 1, :], 0.0)

    for k in range(1, nz):
        arrived(gate_r.at[near[k]], gsem_r.at[near[k]])
    slot_g = gate_r[...].reshape(slots, experts)[:, 0:1].astype(F32)
    hidden_f = hid[...].astype(F32)
    scaled_t = (slot_g * hidden_f).T.astype(BF16)
    hg_s[...] = scaled_t.reshape(hg_s.shape)
    hg_all[me] = hg_s[me]

    relay_near(0)

    for k in range(nz):
        if k:
            landed(k)
            if True:
                spread_own(k)
        score = jnp.sum(gat[me, near[k]].astype(F32) * y[near[k]], axis=1, keepdims=True)
        target = ret_s if k else ret_r
        target[near[k]] = jnp.broadcast_to(score, (cap, tokens))
        if k:
            send(ret_s.at[near[k]], ret_r.at[mz], rs_s.at[k], rs_r.at[mz], (me, near[k]))
    relay_far(0)

    rows = gat[me].reshape(slots, width)
    raw = rows_times(rows, weight[...])
    hidden_v[...] = (slot_g * raw).astype(BF16)
    out_hidden = pltpu.make_async_copy(hidden_v, hidden_o, store_sem.at[0])
    out_hidden.start()

    relay_near(1)
    relay_near(2)
    relay_near(3)

    for k in range(1, nz):
        arrived(ret_r.at[near[k]], rs_r.at[near[k]])
    score_all = rest_all
    for e in range(nz):
        one = jnp.sum(tables[e] * ret_r[e], axis=0, keepdims=True)
        score_all = jnp.where(e_row == e, one, score_all)
    mean = jnp.sum(gate * score_all, axis=0, keepdims=True)
    logit_grad = gate * (score_all - mean)
    lt[...] = logit_grad.astype(BF16)
    lt_all[me] = lt[...]
    for p in TOKEN_ORDER:
        send(lt, lt_all.at[me], lg_s.at[p], lg_r.at[p], (peers[p], mz))
    relay_far(1)
    for p in TOKEN_ORDER:
        send(hg_s.at[peers[p]], hg_all.at[me], hs_s.at[p], hs_r.at[p], (peers[p], mz))
    logit_bf = logit_grad.T.astype(BF16)
    token_v[...] = rows_times(logit_bf, rw[...]).astype(BF16)
    out_token = pltpu.make_async_copy(token_v, token_o, store_sem.at[1])
    out_token.start()

    relay_far(2)
    relay_far(3)

    tok_all[me] = tok[:, pl.ds(pl.multiple_of(me * own_cols, own_cols), own_cols)]
    for p in range(1, nd):
        arrived(tok_all.at[peers[p]], tk_r.at[p])
        arrived(lt_all.at[peers[p]], lg_r.at[p])
    lhs = jnp.concatenate([lt_all[j] for j in range(nd)], axis=1)
    partial = times(lhs, tok_all[...].reshape(nd * tokens, own_cols))
    rg_s[...] = partial.reshape(rg_s.shape).astype(BF16)
    rg_r[mz] = rg_s[mz]
    for k in Z_ORDER:
        send(rg_s.at[near[k]], rg_r.at[mz], zr_s.at[k], zr_r.at[mz], (me, near[k]))

    for p in range(1, nd):
        arrived(hg_all.at[peers[p]], hs_r.at[p])
    for p in (1, 3, 5, 7):
        for k in range(nz):
            arrived(gat.at[peers[p], near[k]], ag_r.at[k, p])
    lhs = jnp.concatenate([hg_all[j] for j in range(nd)], axis=1)
    step = width // 4
    outs = [out_hidden, out_token]
    for n in range(4):
        cols = slice(n * step, (n + 1) * step)
        down_v[:, cols] = times(lhs, gat[:, :, :, cols].reshape(nd * slots, step))
        out = pltpu.make_async_copy(down_v.at[:, cols], down_o.at[:, cols], store_sem.at[3 + n])
        out.start()
        outs.append(out)

    for k in range(1, nz):
        arrived(rg_r.at[near[k]], zr_r.at[near[k]])
    total = rg_r[0].astype(F32)
    for k in range(1, nz):
        total = total + rg_r[k].astype(F32)
    router_v[...] = total
    out = pltpu.make_async_copy(router_v, router_o, store_sem.at[2])
    out.start()
    outs.append(out)
    for copy in sent:
        copy.wait_send()
    for out in outs:
        out.wait()


def out_kernel(count, *refs):
    sem = refs[-1]
    copies = [pltpu.make_async_copy(refs[i], refs[count + i], sem.at[i]) for i in range(count)]
    for copy in copies:
        copy.start()
    for copy in copies:
        copy.wait()


def hand_out(results):
    count = len(results)
    return pl.pallas_call(
        functools.partial(out_kernel, count),
        out_shape=tuple(jax.ShapeDtypeStruct(r.shape, r.dtype) for r in results),
        in_specs=[pl.BlockSpec(memory_space=pl.ANY)] * count,
        out_specs=(pl.BlockSpec(memory_space=pltpu.HBM),) * count,
        scratch_shapes=[pltpu.SemaphoreType.DMA((count,))],
        compiler_params=pltpu.CompilerParams(vmem_limit_bytes=2**20),
    )(*results)


VMEM_BYTES = 67043328
TOKEN_ORDER = (6, 7, 2, 4, 3, 5, 1)
Z_ORDER = (3, 2, 1)


def fused(nd, nz, tokens_in, out_grad, expert_ids, rest_scores, router_weight, down_weight, saved_hidden):
    cap, hidden_units = saved_hidden.shape[3], saved_hidden.shape[4]
    sources = saved_hidden.shape[2]
    tokens, width = tokens_in.shape
    experts = router_weight.shape[1]
    slots = sources * cap
    own_rows, own_cols, own_exp = hidden_units // nd, width // nd, experts // nz
    vm, dma = pltpu.VMEM, pltpu.SemaphoreType.DMA
    scratch = [
        vm((tokens, width), BF16), vm((tokens, width), BF16),
        vm(expert_ids.shape[::-1], jnp.int32), vm(rest_scores.shape[::-1], F32),
        vm((width, experts), BF16), vm((hidden_units, width), BF16), vm((slots, hidden_units), BF16),
        vm((nz, cap, width), BF16), vm((nd, nz, cap, width), BF16), vm((nz, cap, width), F32),
        vm((nz, cap, experts), BF16), vm((nz, cap, experts), BF16),
        vm((nz, cap, tokens), F32), vm((nz, cap, tokens), F32),
        vm((nd, tokens, own_cols), BF16), vm((experts, tokens), BF16), vm((nd, experts, tokens), BF16),
        vm((nd, own_rows, slots), BF16), vm((nd, own_rows, slots), BF16),
        vm((nz, own_exp, own_cols), BF16), vm((nz, own_exp, own_cols), BF16),
        vm((tokens, width), BF16), vm((own_exp, own_cols), F32),
        vm((own_rows, width), F32), vm((slots, hidden_units), BF16),
        dma((7,)), dma((7,)),
        dma((nz,)), dma((nz,)), dma((nz,)), dma((nz,)),
        dma((nz, 7)), dma((nz, 8)), dma((nd,)), dma((nd,)),
        dma((nz,)), dma((nz,)), dma((nd,)), dma((nd,)), dma((nd,)), dma((nd,)), dma((nz,)), dma((nz,)),
    ]
    any_spec = pl.BlockSpec(memory_space=pl.ANY)
    held = 2 * tokens * width + 4 * own_exp * own_cols + 4 * own_rows * width + 2 * slots * hidden_units
    token_grad, router_grad, down_grad, hidden_grad = pl.pallas_call(
        functools.partial(layer_kernel, nd, nz, cap),
        out_shape=(
            pltpu.VMEM((tokens, width), BF16),
            pltpu.VMEM((own_exp, own_cols), F32),
            pltpu.VMEM((own_rows, width), F32),
            pltpu.VMEM((slots, hidden_units), BF16),
        ),
        in_specs=[pl.BlockSpec(memory_space=pltpu.HBM)] * 7,
        out_specs=(any_spec,) * 4,
        scratch_shapes=scratch,
        compiler_params=pltpu.CompilerParams(
            collective_id=0, has_side_effects=True, vmem_limit_bytes=VMEM_BYTES - held
        ),
    )(
        tokens_in, out_grad, expert_ids.T, rest_scores.T, router_weight,
        down_weight[0], saved_hidden.reshape(slots, hidden_units),
    )
    results = (token_grad, router_grad, down_grad, hidden_grad)
    token_grad, router_grad, down_grad, hidden_grad = hand_out(results)
    return token_grad, router_grad.T, down_grad[None], hidden_grad.reshape(saved_hidden.shape)


def body(nd, nz, *args):
    tokens_in, saved_hidden, router_weight = args[0], args[6], args[4]
    slots = saved_hidden.shape[2] * saved_hidden.shape[3]
    gathered = nd * slots * tokens_in.shape[1] * 2
    fits = nd == 8 and gathered <= 16 * 2**20 and saved_hidden.shape[2] == nz
    fits = fits and nz == 4 and (saved_hidden.shape[4] // nd) % 16 == 0
    if fits:
        return fused(nd, nz, *args)
    return shards(*args)


def solution(mesh):
    sizes = dict(mesh.shape)
    return jax.shard_map(
        functools.partial(body, sizes["dp"], sizes["expert"]),
        mesh=mesh,
        in_specs=(
            P(("dp", "expert"), None),
            P(("dp", "expert"), None),
            P(("dp", "expert"), None),
            P(("dp", "expert"), None),
            P(),
            P("expert", None, None),
            P("dp", "expert", None, None, None),
        ),
        out_specs=(
            P(("dp", "expert"), None),
            P("dp", "expert"),
            P("expert", "dp", None),
            P("dp", "expert", None, None, None),
        ),
        check_vma=False,
    )
```

profile of v0, /device:TPU:0, one launch (start us, length us, event | category | flops | bytes accessed | tf_op | source)
XLA Modules:
  0.0 33.6 jit_solution(5536171285739635708)
XLA Ops:
  0.6 31.8 %shard_map.102 = (bf16[128,2048]{1,0:T(8,128)(2,1)S(1)}, f32[32,256]{1,0:T(8,128)S(1)}, f32[96,2048]{1,0:T(8,128)S(1)}, bf16[64,768]{1,0:T(8,128)(2,1)S(1)}) custom-call(bf16[128,2048]{1,0:T(8,128)(2,1)} %tok_h.1, bf16[128,2048]{1,0:T(8,128)(2,1)} %grad_h.1, s32[8,128]{1,0:T(8,128)} %bitcast.9, f32[8,128]{1,0:T(8,128)} %bitcast.10, bf16[2048,128]{1,0:T(8,128)(2,1)} %rw_h.1, ...), custom_call_target="tpu_custom_call" | custom-call | tf_op jit(solution)/shard_map/pallas_call | solution.py:386
  32.5 1.1 %shard_map.103 = (bf16[128,2048]{1,0:T(8,128)(2,1)}, f32[32,256]{1,0:T(8,128)}, f32[96,2048]{1,0:T(8,128)}, bf16[64,768]{1,0:T(8,128)(2,1)}) custom-call(bf16[128,2048]{1,0:T(8,128)(2,1)S(1)} %get-tuple-element.12.refs_0_, f32[32,256]{1,0:T(8,128)S(1)} %get-tuple-element.13.refs_1_, f32[96,2048]{1,0:T(8,128)S(1)} %get-tuple-element.14.refs_2_, ...), custom_call_target="tpu_custom_call" | custom-call | tf_op jit(solution)/shard_map/pallas_call | solution.py:344
where the time goes:
time: 33.8 us; the launch traced here: 33.6 us
  Pallas kernels  33 us (98%)
  between operations  0.64 us (2%)
    pallas_call x1, Pallas kernels, fused(): pl.pallas_call(functools.partial(layer_kernel, nd, nz, cap), out_shape=(p...  31.8 us
    pallas_call x1, Pallas kernels, hand_out(): pl.pallas_call(functools.partial(out_kernel, count), out_shape=tuple((jax...  1.12 us

commit v1 on v0

--- a/solution.py
+++ b/solution.py
@@ -111,10 +111,9 @@
     tok_h, grad_h, ids_h, rest_h, rw_h, w_h, hid_h,
     token_o, router_o, down_o, hidden_o,
     tok, grad, ids, rest, rw, weight, hid,
-    blk, gat, y, gate_s, gate_r, ret_s, ret_r, tok_all, lt, lt_all, hg_s, hg_all, rg_s, rg_r,
-    token_v, router_v, down_v, hidden_v,
-    load_sem, store_sem, disp_s, disp_r, gsem_s, gsem_r, ag_s, ag_r, tk_s, tk_r,
-    rs_s, rs_r, lg_s, lg_r, hs_s, hs_r, zr_s, zr_r,
+    blk, gat, y, gate_s, gate_r, ret_s, ret_r, tok_all, info_s, info_all, sc_s, sc_all,
+    gate_all, base_all, hg_s, hg_all, rg_s, rg_r,
+    load_sem, send_sem, recv_sem, disp_r, near_r, in_r,
 ):
     me = lax.axis_index("dp")
     mz = lax.axis_index("expert")
@@ -132,6 +131,8 @@
         loads[-1].start()
     ld_ids, ld_grad, ld_tok, ld_rw, ld_rest, ld_hid, ld_w = loads
 
+    disp_s, gsem_s, ag_s, tk_s, rs_s, in_s, st_s, hs_s, zr_s = [send_sem.at[i] for i in range(9)]
+    gsem_r, tk_r, rs_r, ina_r, st_r, hs_r, zr_r, core_r, last_r = [recv_sem.at[i] for i in range(9)]
     peers = [flip(me, p) for p in range(nd)]
     half = lax.div(mz, 2)
     near = [mz, mz + 1 - 2 * lax.rem(mz, 2), 2 - half, 3 - 3 * half]
@@ -141,14 +142,10 @@
     for k in range(1, nz):
         pl.semaphore_signal(barrier, inc=1, device_id=(me, near[k]), device_id_type=MESH)
 
-    sent = []
-
     def send(src, dst, s_sem, r_sem, device):
-        copy = pltpu.make_async_remote_copy(
+        pltpu.make_async_remote_copy(
             src_ref=src, dst_ref=dst, send_sem=s_sem, recv_sem=r_sem, device_id=device, device_id_type=MESH
-        )
-        copy.start()
-        sent.append(copy)
+        ).start()
 
     def arrived(ref, r_sem):
         pltpu.make_async_copy(ref, ref, r_sem).wait()
@@ -171,163 +168,207 @@
     table = jnp.concatenate(tables, axis=0).astype(BF16)
 
     ld_grad.wait()
-    for e in range(nz):
-        blk[e] = times(table[e * cap : (e + 1) * cap], grad[...]).astype(BF16)
+    blk[...] = times(table, grad[...]).astype(BF16).reshape(blk.shape)
     gat[me, mz] = blk[mz]
 
     pl.semaphore_wait(barrier, nd - 1 + nz - 1)
     for k in Z_ORDER:
-        send(blk.at[near[k]], gat.at[me, mz], disp_s.at[k], disp_r.at[mz], (me, near[k]))
-
-    def spread(ref, k, origin, target, n):
-        send(ref, ref, ag_s.at[k, n], ag_r.at[k, origin ^ target], (peers[target], mz))
+        send(blk.at[near[k]], gat.at[me, mz], disp_s, disp_r.at[mz], (me, near[k]))
+
+    def spread(ref, k, origin, target):
+        from_p = origin ^ target
+        if from_p % 2 == 0:
+            r_sem = near_r.at[k, from_p // 2]
+        else:
+            r_sem = last_r if from_p == 7 else core_r
+        send(ref, ref, ag_s, r_sem, (peers[target], mz))
 
     def landed(k):
         arrived(gat.at[me, near[k]], disp_r.at[near[k]])
 
     def spread_own(k):
         ref = gat.at[me, near[k]]
-        for n, target in enumerate((2, 4, 1)):
-            spread(ref, k, 0, target, n)
+        for target in (2, 4, 1):
+            spread(ref, k, 0, target)
 
     def relay_near(k):
         via = 2 if k % 2 == 0 else 4
         for origin in (via, 6 - via):
             ref = gat.at[peers[origin], near[k]]
-            arrived(ref, ag_r.at[k, origin])
+            arrived(ref, near_r.at[k, origin // 2])
             if origin == via:
-                spread(ref, k, origin, 6 - via, 3)
-            spread(ref, k, origin, 1, 4 + (origin // 4))
+                spread(ref, k, origin, 6 - via)
+            spread(ref, k, origin, 1)
 
     def relay_far(k):
         ref = gat.at[peers[6], near[k]]
-        arrived(ref, ag_r.at[k, 6])
-        spread(ref, k, 6, 1, 6)
+        arrived(ref, near_r.at[k, 3])
+        spread(ref, k, 6, 1)
 
     spread_own(0)
 
     ld_tok.wait()
-    for p in TOKEN_ORDER:
-        cols = pl.ds(pl.multiple_of(peers[p] * own_cols, own_cols), own_cols)
-        send(tok.at[:, cols], tok_all.at[me], tk_s.at[p], tk_r.at[p], (peers[p], mz))
-
-
     ld_rw.wait()
     logits = times(tok[...], rw[...]).T
     low = jnp.where(mask, logits, -3.0e38)
     raised = jnp.where(mask, jnp.exp(low - jnp.max(low, axis=0, keepdims=True)), 0.0)
     gate = raised / jnp.sum(raised, axis=0, keepdims=True)
+    for k in range(topk):
+        info_s[k : k + 1, :] = jnp.sum(jnp.where(hits[k], gate, 0.0), axis=0, keepdims=True)
+    ld_rest.wait()
+    restv = rest[...]
+    info_s[topk : 2 * topk, :] = restv
+    info_s[2 * topk : 3 * topk, :] = idv.astype(F32)
     for e in range(nz):
         one = jnp.sum(tables[e] * gate[e : e + 1, :], axis=1, keepdims=True)
         gate_s[e] = jnp.broadcast_to(one, (cap, experts)).astype(BF16)
     gate_r[mz] = gate_s[mz]
     for k in range(1, nz):
-        send(gate_s.at[near[k]], gate_r.at[mz], gsem_s.at[k], gsem_r.at[mz], (me, near[k]))
+        send(gate_s.at[near[k]], gate_r.at[mz], gsem_s, gsem_r, (me, near[k]))
+    for p in (6, 2, 4, 1):
+        send(info_s, info_all.at[me], in_s, in_r.at[p // 2] if p > 1 else ina_r, (peers[p], mz))
+    for p in TOKEN_ORDER:
+        cols = pl.ds(pl.multiple_of(peers[p] * own_cols, own_cols), own_cols)
+        send(tok.at[:, cols], tok_all.at[me], tk_s, tk_r, (peers[p], mz))
 
     ld_hid.wait()
     ld_w.wait()
     y[...] = times(hid[...], weight[...]).reshape(y.shape)
 
-    ld_rest.wait()
-    restv = rest[...]
+    outside = e_row >= nz
+
+    def expand(j, g, r):
+        r = jnp.where(outside, r, 0.0)
+        gate_all[j] = g
+        base_all[j] = g * (r - jnp.sum(g * r, axis=0, keepdims=True))
+
     rest_all = jnp.where(hits[0], restv[0:1, :], 0.0)
     for k in range(1, topk):
-        rest_all = rest_all + jnp.where(hits[k], restv[k : k + 1, :], 0.0)
-
-    for k in range(1, nz):
-        arrived(gate_r.at[near[k]], gsem_r.at[near[k]])
+        rest_all = jnp.where(hits[k], restv[k : k + 1, :], rest_all)
+    expand(me, gate, rest_all)
+    tok_all[me] = tok[:, pl.ds(pl.multiple_of(me * own_cols, own_cols), own_cols)]
+
+    def score_of(k):
+        score = jnp.sum(gat[me, near[k]].astype(F32) * y[near[k]], axis=1, keepdims=True)
+        target = ret_s if k else ret_r
+        target[near[k]] = jnp.broadcast_to(score, (cap, tokens))
+        if k:
+            send(ret_s.at[near[k]], ret_r.at[mz], rs_s, rs_r, (me, near[k]))
+
+    score_of(0)
+    landed(1)
+    score_of(1)
+    spread_own(1)
+    relay_near(0)
+    landed(2)
+    score_of(2)
+    spread_own(2)
+    landed(3)
+    score_of(3)
+    if not LATE_SPREAD:
+        spread_own(3)
+    arrived(gate_r.at[1:nz], gsem_r)
     slot_g = gate_r[...].reshape(slots, experts)[:, 0:1].astype(F32)
     hidden_f = hid[...].astype(F32)
     scaled_t = (slot_g * hidden_f).T.astype(BF16)
     hg_s[...] = scaled_t.reshape(hg_s.shape)
     hg_all[me] = hg_s[me]
 
-    relay_near(0)
-
-    for k in range(nz):
-        if k:
-            landed(k)
-            if True:
-                spread_own(k)
-        score = jnp.sum(gat[me, near[k]].astype(F32) * y[near[k]], axis=1, keepdims=True)
-        target = ret_s if k else ret_r
-        target[near[k]] = jnp.broadcast_to(score, (cap, tokens))
-        if k:
-            send(ret_s.at[near[k]], ret_r.at[mz], rs_s.at[k], rs_r.at[mz], (me, near[k]))
-    relay_far(0)
-
-    rows = gat[me].reshape(slots, width)
-    raw = rows_times(rows, weight[...])
-    hidden_v[...] = (slot_g * raw).astype(BF16)
-    out_hidden = pltpu.make_async_copy(hidden_v, hidden_o, store_sem.at[0])
-    out_hidden.start()
-
+    for p in (2, 4, 6):
+        ref = info_all.at[peers[p]]
+        arrived(ref, in_r.at[p // 2])
+        send(ref, ref, in_s, ina_r, (peers[1], mz))
+    e_rowf = e_row.astype(F32)
+    for p in (2, 4, 6, 1, 3, 5, 7):
+        j = peers[p]
+        if p == 1:
+            arrived(info_all.at[0:4], ina_r)
+        g = jnp.zeros((experts, tokens), F32)
+        r = g
+        for k in range(topk):
+            hit = info_all[j, 2 * topk + k : 2 * topk + k + 1, :] == e_rowf
+            g = jnp.where(hit, info_all[j, k : k + 1, :], g)
+            r = jnp.where(hit, info_all[j, topk + k : topk + k + 1, :], r)
+        expand(j, g, r)
+
+    arrived(ret_r.at[1:nz], rs_r)
+    for e in range(nz):
+        sc_s[e : e + 1, :] = jnp.sum(tables[e] * ret_r[e], axis=0, keepdims=True)
+    for p in TOKEN_ORDER:
+        send(sc_s, sc_all.at[me], st_s, st_r, (peers[p], mz))
+    if LATE_SPREAD:
+        spread_own(3)
+    for p in TOKEN_ORDER:
+        send(hg_s.at[peers[p]], hg_all.at[me], hs_s, hs_r, (peers[p], mz))
+
+    def logit_grad(j, score):
+        g = gate_all[j]
+        mean = jnp.sum(g[0:nz, :] * score, axis=0, keepdims=True)
+        late = base_all[j] - g * mean
+        for e in range(nz):
+            late = late + jnp.where(e_row == e, g * score[e : e + 1, :], 0.0)
+        return late
+
+    def hidden_part(n, parts):
+        step = hidden_units // parts
+        raw = rows_times(gat[me].reshape(slots, width), weight[n * step : (n + 1) * step, :])
+        hidden_o[:, n * step : (n + 1) * step] = (slot_g * raw).astype(BF16)
+
+    own_grad = logit_grad(me, sc_s[0:nz, :])
+    token_o[...] = rows_times(own_grad.T.astype(BF16), rw[...]).astype(BF16)
     relay_near(1)
     relay_near(2)
+    relay_far(0)
     relay_near(3)
-
-    for k in range(1, nz):
-        arrived(ret_r.at[near[k]], rs_r.at[near[k]])
-    score_all = rest_all
-    for e in range(nz):
-        one = jnp.sum(tables[e] * ret_r[e], axis=0, keepdims=True)
-        score_all = jnp.where(e_row == e, one, score_all)
-    mean = jnp.sum(gate * score_all, axis=0, keepdims=True)
-    logit_grad = gate * (score_all - mean)
-    lt[...] = logit_grad.astype(BF16)
-    lt_all[me] = lt[...]
-    for p in TOKEN_ORDER:
-        send(lt, lt_all.at[me], lg_s.at[p], lg_r.at[p], (peers[p], mz))
-    relay_far(1)
-    for p in TOKEN_ORDER:
-        send(hg_s.at[peers[p]], hg_all.at[me], hs_s.at[p], hs_r.at[p], (peers[p], mz))
-    logit_bf = logit_grad.T.astype(BF16)
-    token_v[...] = rows_times(logit_bf, rw[...]).astype(BF16)
-    out_token = pltpu.make_async_copy(token_v, token_o, store_sem.at[1])
-    out_token.start()
-
-    relay_far(2)
-    relay_far(3)
-
-    tok_all[me] = tok[:, pl.ds(pl.multiple_of(me * own_cols, own_cols), own_cols)]
+    arrived(sc_all.at[1:nd], st_r)
+    grads = [own_grad.astype(BF16)]
     for p in range(1, nd):
-        arrived(tok_all.at[peers[p]], tk_r.at[p])
-        arrived(lt_all.at[peers[p]], lg_r.at[p])
-    lhs = jnp.concatenate([lt_all[j] for j in range(nd)], axis=1)
-    partial = times(lhs, tok_all[...].reshape(nd * tokens, own_cols))
+        grads.append(logit_grad(peers[p], sc_all[peers[p], 0:nz, :]).astype(BF16))
+    arrived(tok_all.at[1:nd], tk_r)
+    lhs = jnp.concatenate(grads, axis=1)
+    rhs = jnp.concatenate([tok_all[peers[p]] for p in range(nd)], axis=0)
+    partial = times(lhs, rhs)
     rg_s[...] = partial.reshape(rg_s.shape).astype(BF16)
     rg_r[mz] = rg_s[mz]
     for k in Z_ORDER:
-        send(rg_s.at[near[k]], rg_r.at[mz], zr_s.at[k], zr_r.at[mz], (me, near[k]))
-
-    for p in range(1, nd):
-        arrived(hg_all.at[peers[p]], hs_r.at[p])
-    for p in (1, 3, 5, 7):
-        for k in range(nz):
-            arrived(gat.at[peers[p], near[k]], ag_r.at[k, p])
-    lhs = jnp.concatenate([hg_all[j] for j in range(nd)], axis=1)
-    step = width // 4
-    outs = [out_hidden, out_token]
-    for n in range(4):
-        cols = slice(n * step, (n + 1) * step)
-        down_v[:, cols] = times(lhs, gat[:, :, :, cols].reshape(nd * slots, step))
-        out = pltpu.make_async_copy(down_v.at[:, cols], down_o.at[:, cols], store_sem.at[3 + n])
-        out.start()
-        outs.append(out)
-
-    for k in range(1, nz):
-        arrived(rg_r.at[near[k]], zr_r.at[near[k]])
+        send(rg_s.at[near[k]], rg_r.at[mz], zr_s, zr_r, (me, near[k]))
+    hidden_part(0, 3)
+    relay_far(1)
+    hidden_part(1, 3)
+    relay_far(2)
+    hidden_part(2, 3)
+    relay_far(3)
+
+    arrived(hg_all.at[1:nd], hs_r)
+    arrived(gat.at[0:3], core_r)
+
+    def down_part(group, first):
+        lhs = jnp.concatenate([hg_all[peers[p]] for p in group], axis=1)
+        step = width // 4
+        for n in range(4):
+            cols = slice(n * step, (n + 1) * step)
+            rhs = jnp.concatenate([gat[peers[p], :, :, cols].reshape(slots, step) for p in group], axis=0)
+            part = times(lhs, rhs)
+            down_o[:, cols] = part if first else down_o[:, cols] + part
+
+    down_part(range(0, 4), True)
+    arrived(gat.at[0], last_r)
+    down_part(range(4, 8), False)
+
+    arrived(rg_r.at[1:nz], zr_r)
     total = rg_r[0].astype(F32)
     for k in range(1, nz):
         total = total + rg_r[k].astype(F32)
-    router_v[...] = total
-    out = pltpu.make_async_copy(router_v, router_o, store_sem.at[2])
-    out.start()
-    outs.append(out)
-    for copy in sent:
-        copy.wait_send()
-    for out in outs:
-        out.wait()
+    router_o[...] = total
+    arrived(blk.at[1:nz], disp_s)
+    arrived(gate_s.at[1:nz], gsem_s)
+    arrived(gat.at[1:nd], ag_s)
+    arrived(tok_all.at[1:nd], tk_s)
+    arrived(ret_s.at[1:nz], rs_s)
+    arrived(info_all.at[1:nd], in_s)
+    arrived(sc_all.at[1:nd], st_s)
+    arrived(hg_s.at[1:nd], hs_s)
+    arrived(rg_s.at[1:nz], zr_s)
 
 
 def out_kernel(count, *refs):
@@ -354,6 +395,7 @@
 VMEM_BYTES = 67043328
 TOKEN_ORDER = (6, 7, 2, 4, 3, 5, 1)
 Z_ORDER = (3, 2, 1)
+LATE_SPREAD = True
 
 
 def fused(nd, nz, tokens_in, out_grad, expert_ids, rest_scores, router_weight, down_weight, saved_hidden):
@@ -361,6 +403,7 @@
     sources = saved_hidden.shape[2]
     tokens, width = tokens_in.shape
     experts = router_weight.shape[1]
+    topk = expert_ids.shape[1]
     slots = sources * cap
     own_rows, own_cols, own_exp = hidden_units // nd, width // nd, experts // nz
     vm, dma = pltpu.VMEM, pltpu.SemaphoreType.DMA
@@ -371,17 +414,15 @@
         vm((nz, cap, width), BF16), vm((nd, nz, cap, width), BF16), vm((nz, cap, width), F32),
         vm((nz, cap, experts), BF16), vm((nz, cap, experts), BF16),
         vm((nz, cap, tokens), F32), vm((nz, cap, tokens), F32),
-        vm((nd, tokens, own_cols), BF16), vm((experts, tokens), BF16), vm((nd, experts, tokens), BF16),
+        vm((nd, tokens, own_cols), BF16),
+        vm((3 * topk, tokens), F32), vm((nd, 3 * topk, tokens), F32),
+        vm((nz, tokens), F32), vm((nd, nz, tokens), F32),
+        vm((nd, experts, tokens), F32), vm((nd, experts, tokens), F32),
         vm((nd, own_rows, slots), BF16), vm((nd, own_rows, slots), BF16),
         vm((nz, own_exp, own_cols), BF16), vm((nz, own_exp, own_cols), BF16),
-        vm((tokens, width), BF16), vm((own_exp, own_cols), F32),
-        vm((own_rows, width), F32), vm((slots, hidden_units), BF16),
-        dma((7,)), dma((7,)),
-        dma((nz,)), dma((nz,)), dma((nz,)), dma((nz,)),
-        dma((nz, 7)), dma((nz, 8)), dma((nd,)), dma((nd,)),
-        dma((nz,)), dma((nz,)), dma((nd,)), dma((nd,)), dma((nd,)), dma((nd,)), dma((nz,)), dma((nz,)),
+        dma((7,)), dma((9,)), dma((9,)), dma((nz,)), dma((nz, nz)), dma((nz,)),
     ]
-    any_spec = pl.BlockSpec(memory_space=pl.ANY)
+    vm_spec = pl.BlockSpec(memory_space=pltpu.VMEM)
     held = 2 * tokens * width + 4 * own_exp * own_cols + 4 * own_rows * width + 2 * slots * hidden_units
     token_grad, router_grad, down_grad, hidden_grad = pl.pallas_call(
         functools.partial(layer_kernel, nd, nz, cap),
@@ -392,7 +433,7 @@
             pltpu.VMEM((slots, hidden_units), BF16),
         ),
         in_specs=[pl.BlockSpec(memory_space=pltpu.HBM)] * 7,
-        out_specs=(any_spec,) * 4,
+        out_specs=(vm_spec,) * 4,
         scratch_shapes=scratch,
         compiler_params=pltpu.CompilerParams(
             collective_id=0, has_side_effects=True, vmem_limit_bytes=VMEM_BYTES - held

time: 33.8 us -> 29.7 us (0.88)
  Pallas kernels: 33 us -> 28.5 us
    pallas_call x1, Pallas kernels: 31.8 us -> 27.4 us  [fused(): pl.pallas_call(functools.partial(layer_kernel, nd, nz, cap), out_shape=(p...]
where the time goes in v1:
time: 29.7 us; the launch traced here: 29.2 us
  Pallas kernels  28.5 us (96%)
  between operations  0.64 us (2%)
    pallas_call x1, Pallas kernels, fused(): pl.pallas_call(functools.partial(layer_kernel, nd, nz, cap), out_shape=(p...  27.4 us
    pallas_call x1, Pallas kernels, hand_out(): pl.pallas_call(functools.partial(out_kernel, count), out_shape=tuple((jax...  1.12 us

profile of v1, /device:TPU:0, one launch (start us, length us, event | category | flops | bytes accessed | tf_op | source)
XLA Modules:
  0.0 29.2 jit_solution(14463319860057529220)
XLA Ops:
  0.6 27.4 %shard_map.102 = (bf16[128,2048]{1,0:T(8,128)(2,1)S(1)}, f32[32,256]{1,0:T(8,128)S(1)}, f32[96,2048]{1,0:T(8,128)S(1)}, bf16[64,768]{1,0:T(8,128)(2,1)S(1)}) custom-call(bf16[128,2048]{1,0:T(8,128)(2,1)} %tok_h.1, bf16[128,2048]{1,0:T(8,128)(2,1)} %grad_h.1, s32[8,128]{1,0:T(8,128)} %bitcast.9, f32[8,128]{1,0:T(8,128)} %bitcast.10, bf16[2048,128]{1,0:T(8,128)(2,1)} %rw_h.1, ...), custom_call_target="tpu_custom_call" | custom-call | tf_op jit(solution)/shard_map/pallas_call | solution.py:427
  28.1 1.1 %shard_map.103 = (bf16[128,2048]{1,0:T(8,128)(2,1)}, f32[32,256]{1,0:T(8,128)}, f32[96,2048]{1,0:T(8,128)}, bf16[64,768]{1,0:T(8,128)(2,1)}) custom-call(bf16[128,2048]{1,0:T(8,128)(2,1)S(1)} %get-tuple-element.12.refs_0_, f32[32,256]{1,0:T(8,128)S(1)} %get-tuple-element.13.refs_1_, f32[96,2048]{1,0:T(8,128)S(1)} %get-tuple-element.14.refs_2_, ...), custom_call_target="tpu_custom_call" | custom-call | tf_op jit(solution)/shard_map/pallas_call | solution.py:385

commit v2 on v1

--- a/solution.py
+++ b/solution.py
@@ -106,13 +106,20 @@
     return lax.dot_general(a, b, (((1,), (0,)), ((), ())), preferred_element_type=F32)
 
 
+def down_part(group, gat, hg_all, cols):
+    lhs = jnp.concatenate([hg_all[j] for j in group], axis=1)
+    slots = lhs.shape[1] // len(group)
+    rhs = jnp.concatenate([gat[j, :, :, cols].reshape(slots, -1) for j in group], axis=0)
+    return times(lhs, rhs)
+
+
 def layer_kernel(
     nd, nz, cap,
     tok_h, grad_h, ids_h, rest_h, rw_h, w_h, hid_h,
-    token_o, router_o, down_o, hidden_o,
+    token_o, router_o, down_o, hidden_o, gat, hg_all,
     tok, grad, ids, rest, rw, weight, hid,
-    blk, gat, y, gate_s, gate_r, ret_s, ret_r, tok_all, info_s, info_all, sc_s, sc_all,
-    gate_all, base_all, hg_s, hg_all, rg_s, rg_r,
+    blk, y, gate_s, gate_r, ret_s, ret_r, tok_all, info_s, info_all, sc_s, sc_all,
+    gate_all, base_all, hg_s, rg_s, rg_r,
     load_sem, send_sem, recv_sem, disp_r, near_r, in_r,
 ):
     me = lax.axis_index("dp")
@@ -130,7 +137,6 @@
         loads.append(pltpu.make_async_copy(src, dst, load_sem.at[i]))
         loads[-1].start()
     ld_ids, ld_grad, ld_tok, ld_rw, ld_rest, ld_hid, ld_w = loads
-
     disp_s, gsem_s, ag_s, tk_s, rs_s, in_s, st_s, hs_s, zr_s = [send_sem.at[i] for i in range(9)]
     gsem_r, tk_r, rs_r, ina_r, st_r, hs_r, zr_r, core_r, last_r = [recv_sem.at[i] for i in range(9)]
     peers = [flip(me, p) for p in range(nd)]
@@ -141,6 +147,7 @@
         pl.semaphore_signal(barrier, inc=1, device_id=(peers[p], mz), device_id_type=MESH)
     for k in range(1, nz):
         pl.semaphore_signal(barrier, inc=1, device_id=(me, near[k]), device_id_type=MESH)
+
 
     def send(src, dst, s_sem, r_sem, device):
         pltpu.make_async_remote_copy(
@@ -175,10 +182,21 @@
     for k in Z_ORDER:
         send(blk.at[near[k]], gat.at[me, mz], disp_s, disp_r.at[mz], (me, near[k]))
 
-    def spread(ref, k, origin, target):
+    def pieces(k):
+        parts = 2 if k in SPLIT else 1
+        return [(h, pl.ds(h * (width // parts), width // parts)) for h in range(parts)]
+
+    def via_of(k, h):
+        return 4 if (k + h) % 2 else 2
+
+    def near_sem(k, origin, h):
+        return near_r.at[SLOT[k, origin, h]]
+
+    def spread(k, h, cols, origin, target):
         from_p = origin ^ target
+        ref = gat.at[peers[origin], near[k], :, cols]
         if from_p % 2 == 0:
-            r_sem = near_r.at[k, from_p // 2]
+            r_sem = near_sem(k, from_p, h)
         else:
             r_sem = last_r if from_p == 7 else core_r
         send(ref, ref, ag_s, r_sem, (peers[target], mz))
@@ -187,23 +205,24 @@
         arrived(gat.at[me, near[k]], disp_r.at[near[k]])
 
     def spread_own(k):
-        ref = gat.at[me, near[k]]
-        for target in (2, 4, 1):
-            spread(ref, k, 0, target)
-
-    def relay_near(k):
-        via = 2 if k % 2 == 0 else 4
-        for origin in (via, 6 - via):
-            ref = gat.at[peers[origin], near[k]]
-            arrived(ref, near_r.at[k, origin // 2])
-            if origin == via:
-                spread(ref, k, origin, 6 - via)
-            spread(ref, k, origin, 1)
-
-    def relay_far(k):
-        ref = gat.at[peers[6], near[k]]
-        arrived(ref, near_r.at[k, 3])
-        spread(ref, k, 6, 1)
+        for h, cols in pieces(k):
+            via = via_of(k, h)
+            for target in (via, 6 - via):
+                spread(k, h, cols, 0, target)
+        for h, cols in pieces(k):
+            spread(k, h, cols, 0, 1)
+
+    def relay_via(k, h):
+        cols = pieces(k)[h][1]
+        via = via_of(k, h)
+        arrived(gat.at[peers[via], near[k], :, cols], near_sem(k, via, h))
+        spread(k, h, cols, via, 6 - via)
+        spread(k, h, cols, via, 1)
+
+    def relay_core(k, h, origin):
+        cols = pieces(k)[h][1]
+        arrived(gat.at[peers[origin], near[k], :, cols], near_sem(k, origin, h))
+        spread(k, h, cols, origin, 1)
 
     spread_own(0)
 
@@ -227,9 +246,12 @@
         send(gate_s.at[near[k]], gate_r.at[mz], gsem_s, gsem_r, (me, near[k]))
     for p in (6, 2, 4, 1):
         send(info_s, info_all.at[me], in_s, in_r.at[p // 2] if p > 1 else ina_r, (peers[p], mz))
-    for p in TOKEN_ORDER:
+    def send_tokens(p):
         cols = pl.ds(pl.multiple_of(peers[p] * own_cols, own_cols), own_cols)
         send(tok.at[:, cols], tok_all.at[me], tk_s, tk_r, (peers[p], mz))
+
+    for p in EARLY_TOKENS:
+        send_tokens(p)
 
     ld_hid.wait()
     ld_w.wait()
@@ -254,52 +276,6 @@
         target[near[k]] = jnp.broadcast_to(score, (cap, tokens))
         if k:
             send(ret_s.at[near[k]], ret_r.at[mz], rs_s, rs_r, (me, near[k]))
-
-    score_of(0)
-    landed(1)
-    score_of(1)
-    spread_own(1)
-    relay_near(0)
-    landed(2)
-    score_of(2)
-    spread_own(2)
-    landed(3)
-    score_of(3)
-    if not LATE_SPREAD:
-        spread_own(3)
-    arrived(gate_r.at[1:nz], gsem_r)
-    slot_g = gate_r[...].reshape(slots, experts)[:, 0:1].astype(F32)
-    hidden_f = hid[...].astype(F32)
-    scaled_t = (slot_g * hidden_f).T.astype(BF16)
-    hg_s[...] = scaled_t.reshape(hg_s.shape)
-    hg_all[me] = hg_s[me]
-
-    for p in (2, 4, 6):
-        ref = info_all.at[peers[p]]
-        arrived(ref, in_r.at[p // 2])
-        send(ref, ref, in_s, ina_r, (peers[1], mz))
-    e_rowf = e_row.astype(F32)
-    for p in (2, 4, 6, 1, 3, 5, 7):
-        j = peers[p]
-        if p == 1:
-            arrived(info_all.at[0:4], ina_r)
-        g = jnp.zeros((experts, tokens), F32)
-        r = g
-        for k in range(topk):
-            hit = info_all[j, 2 * topk + k : 2 * topk + k + 1, :] == e_rowf
-            g = jnp.where(hit, info_all[j, k : k + 1, :], g)
-            r = jnp.where(hit, info_all[j, topk + k : topk + k + 1, :], r)
-        expand(j, g, r)
-
-    arrived(ret_r.at[1:nz], rs_r)
-    for e in range(nz):
-        sc_s[e : e + 1, :] = jnp.sum(tables[e] * ret_r[e], axis=0, keepdims=True)
-    for p in TOKEN_ORDER:
-        send(sc_s, sc_all.at[me], st_s, st_r, (peers[p], mz))
-    if LATE_SPREAD:
-        spread_own(3)
-    for p in TOKEN_ORDER:
-        send(hg_s.at[peers[p]], hg_all.at[me], hs_s, hs_r, (peers[p], mz))
 
     def logit_grad(j, score):
         g = gate_all[j]
@@ -311,50 +287,119 @@
 
     def hidden_part(n, parts):
         step = hidden_units // parts
+        slot_g = gate_r[...].reshape(slots, experts)[:, 0:1].astype(F32)
         raw = rows_times(gat[me].reshape(slots, width), weight[n * step : (n + 1) * step, :])
         hidden_o[:, n * step : (n + 1) * step] = (slot_g * raw).astype(BF16)
 
-    own_grad = logit_grad(me, sc_s[0:nz, :])
-    token_o[...] = rows_times(own_grad.T.astype(BF16), rw[...]).astype(BF16)
-    relay_near(1)
-    relay_near(2)
-    relay_far(0)
-    relay_near(3)
-    arrived(sc_all.at[1:nd], st_r)
-    grads = [own_grad.astype(BF16)]
-    for p in range(1, nd):
-        grads.append(logit_grad(peers[p], sc_all[peers[p], 0:nz, :]).astype(BF16))
-    arrived(tok_all.at[1:nd], tk_r)
-    lhs = jnp.concatenate(grads, axis=1)
-    rhs = jnp.concatenate([tok_all[peers[p]] for p in range(nd)], axis=0)
-    partial = times(lhs, rhs)
-    rg_s[...] = partial.reshape(rg_s.shape).astype(BF16)
-    rg_r[mz] = rg_s[mz]
-    for k in Z_ORDER:
-        send(rg_s.at[near[k]], rg_r.at[mz], zr_s, zr_r, (me, near[k]))
+    def gates_in():
+        arrived(gate_r.at[1:nz], gsem_r)
+        slot_g = gate_r[...].reshape(slots, experts)[:, 0:1].astype(F32)
+        hidden_f = hid[...].astype(F32)
+        scaled_t = (slot_g * hidden_f).T.astype(BF16)
+        hg_s[...] = scaled_t.reshape(hg_s.shape)
+        hg_all[me] = hg_s[me]
+
+    def facts_on():
+        for p in (2, 4, 6):
+            ref = info_all.at[peers[p]]
+            arrived(ref, in_r.at[p // 2])
+            send(ref, ref, in_s, ina_r, (peers[1], mz))
+
+    def facts_in():
+        e_rowf = e_row.astype(F32)
+        for p in (2, 4, 6, 1, 3, 5, 7):
+            j = peers[p]
+            if p == 1:
+                arrived(info_all.at[0:4], ina_r)
+            g = jnp.zeros((experts, tokens), F32)
+            r = g
+            for k in range(topk):
+                hit = info_all[j, 2 * topk + k : 2 * topk + k + 1, :] == e_rowf
+                g = jnp.where(hit, info_all[j, k : k + 1, :], g)
+                r = jnp.where(hit, info_all[j, topk + k : topk + k + 1, :], r)
+            expand(j, g, r)
+
+    def scores_out():
+        arrived(ret_r.at[1:nz], rs_r)
+        for e in range(nz):
+            sc_s[e : e + 1, :] = jnp.sum(tables[e] * ret_r[e], axis=0, keepdims=True)
+        for p in TOKEN_ORDER:
+            send(sc_s, sc_all.at[me], st_s, st_r, (peers[p], mz))
+
+    def hidden_out():
+        for p in TOKEN_ORDER:
+            send(hg_s.at[peers[p]], hg_all.at[me], hs_s, hs_r, (peers[p], mz))
+
+    def token_part():
+        own_grad = logit_grad(me, sc_s[0:nz, :])
+        token_o[...] = rows_times(own_grad.T.astype(BF16), rw[...]).astype(BF16)
+
+    def router_part():
+        arrived(sc_all.at[1:nd], st_r)
+        grads = [logit_grad(me, sc_s[0:nz, :]).astype(BF16)]
+        for p in range(1, nd):
+            grads.append(logit_grad(peers[p], sc_all[peers[p], 0:nz, :]).astype(BF16))
+        arrived(tok_all.at[1:nd], tk_r)
+        lhs = jnp.concatenate(grads, axis=1)
+        rhs = jnp.concatenate([tok_all[peers[p]] for p in range(nd)], axis=0)
+        partial = times(lhs, rhs)
+        rg_s[...] = partial.reshape(rg_s.shape).astype(BF16)
+        rg_r[mz] = rg_s[mz]
+        for k in Z_ORDER:
+            send(rg_s.at[near[k]], rg_r.at[mz], zr_s, zr_r, (me, near[k]))
+
+    score_of(0)
+    landed(1)
+    score_of(1)
+    spread_own(1)
+    relay_via(0, 0)
+    relay_via(0, 1)
+    relay_core(0, 0, 6 - via_of(0, 0))
+    relay_core(0, 1, 6 - via_of(0, 1))
+    landed(2)
+    score_of(2)
+    spread_own(2)
+    landed(3)
+    score_of(3)
+    facts_on()
+    gates_in()
     hidden_part(0, 3)
-    relay_far(1)
     hidden_part(1, 3)
-    relay_far(2)
+    scores_out()
+    spread_own(3)
+    hidden_out()
+    relay_via(1, 0)
+    relay_via(1, 1)
+    relay_core(1, 0, 6 - via_of(1, 0))
+    relay_core(1, 1, 6 - via_of(1, 1))
+    relay_core(0, 0, 6)
+    relay_core(0, 1, 6)
+    facts_in()
+    relay_via(2, 0)
+    relay_via(2, 1)
+    relay_core(2, 0, 6 - via_of(2, 0))
+    relay_core(2, 1, 6 - via_of(2, 1))
     hidden_part(2, 3)
-    relay_far(3)
-
+    router_part()
+    relay_via(3, 0)
+    relay_via(3, 1)
+    relay_core(3, 0, 6 - via_of(3, 0))
+    relay_core(3, 1, 6 - via_of(3, 1))
+    relay_core(1, 0, 6)
+    relay_core(1, 1, 6)
+    relay_core(2, 0, 6)
+    relay_core(2, 1, 6)
+    token_part()
+    relay_core(3, 0, 6)
+    relay_core(3, 1, 6)
     arrived(hg_all.at[1:nd], hs_r)
     arrived(gat.at[0:3], core_r)
 
-    def down_part(group, first):
-        lhs = jnp.concatenate([hg_all[peers[p]] for p in group], axis=1)
-        step = width // 4
-        for n in range(4):
-            cols = slice(n * step, (n + 1) * step)
-            rhs = jnp.concatenate([gat[peers[p], :, :, cols].reshape(slots, step) for p in group], axis=0)
-            part = times(lhs, rhs)
-            down_o[:, cols] = part if first else down_o[:, cols] + part
-
-    down_part(range(0, 4), True)
+    step = width // 4
+    for n in range(4):
+        cols = slice(n * step, (n + 1) * step)
+        down_o[:, cols] = down_part(peers[0 : nd // 2], gat, hg_all, cols)
     arrived(gat.at[0], last_r)
-    down_part(range(4, 8), False)
-
     arrived(rg_r.at[1:nz], zr_r)
     total = rg_r[0].astype(F32)
     for k in range(1, nz):
@@ -371,31 +416,52 @@
     arrived(rg_s.at[1:nz], zr_s)
 
 
-def out_kernel(count, *refs):
-    sem = refs[-1]
-    copies = [pltpu.make_async_copy(refs[i], refs[count + i], sem.at[i]) for i in range(count)]
-    for copy in copies:
-        copy.start()
+def out_kernel(nd, token, router, down, hidden, gat, hg_all, token_h, router_h, down_h, hidden_h, total, sem):
+    copies = []
+
+    def put(src, dst):
+        copies.append(pltpu.make_async_copy(src, dst, sem.at[len(copies)]))
+        copies[-1].start()
+
+    put(token, token_h)
+    put(hidden, hidden_h)
+    put(router, router_h)
+    me = lax.axis_index("dp")
+    group = [flip(me, p) for p in range(nd // 2, nd)]
+    step = down.shape[1] // DOWN_STEPS
+    for n in range(DOWN_STEPS):
+        cols = slice(n * step, (n + 1) * step)
+        total[:, cols] = down[:, cols] + down_part(group, gat, hg_all, cols)
+        put(total.at[:, cols], down_h.at[:, cols])
     for copy in copies:
         copy.wait()
 
 
-def hand_out(results):
-    count = len(results)
+def hand_out(nd, results):
+    count = 4
     return pl.pallas_call(
-        functools.partial(out_kernel, count),
-        out_shape=tuple(jax.ShapeDtypeStruct(r.shape, r.dtype) for r in results),
-        in_specs=[pl.BlockSpec(memory_space=pl.ANY)] * count,
+        functools.partial(out_kernel, nd),
+        out_shape=tuple(jax.ShapeDtypeStruct(r.shape, r.dtype) for r in results[:count]),
+        in_specs=[pl.BlockSpec(memory_space=pltpu.VMEM)] * len(results),
         out_specs=(pl.BlockSpec(memory_space=pltpu.HBM),) * count,
-        scratch_shapes=[pltpu.SemaphoreType.DMA((count,))],
-        compiler_params=pltpu.CompilerParams(vmem_limit_bytes=2**20),
+        scratch_shapes=[
+            pltpu.VMEM(results[2].shape, results[2].dtype), pltpu.SemaphoreType.DMA((3 + DOWN_STEPS,))
+        ],
+        compiler_params=pltpu.CompilerParams(vmem_limit_bytes=2**23),
     )(*results)
 
 
+DOWN_STEPS = 4
 VMEM_BYTES = 67043328
 TOKEN_ORDER = (6, 7, 2, 4, 3, 5, 1)
 Z_ORDER = (3, 2, 1)
-LATE_SPREAD = True
+EARLY_TOKENS = (1, 7, 2, 4, 3, 5, 6)
+SPLIT = (0, 1, 2, 3)
+SLOT = {}
+for piece in range(4):
+    for place in (2, 4, 6):
+        for part in range(2 if piece in SPLIT else 1):
+            SLOT[piece, place, part] = len(SLOT)
 
 
 def fused(nd, nz, tokens_in, out_grad, expert_ids, rest_scores, router_weight, down_weight, saved_hidden):
@@ -411,29 +477,32 @@
         vm((tokens, width), BF16), vm((tokens, width), BF16),
         vm(expert_ids.shape[::-1], jnp.int32), vm(rest_scores.shape[::-1], F32),
         vm((width, experts), BF16), vm((hidden_units, width), BF16), vm((slots, hidden_units), BF16),
-        vm((nz, cap, width), BF16), vm((nd, nz, cap, width), BF16), vm((nz, cap, width), F32),
+        vm((nz, cap, width), BF16), vm((nz, cap, width), F32),
         vm((nz, cap, experts), BF16), vm((nz, cap, experts), BF16),
         vm((nz, cap, tokens), F32), vm((nz, cap, tokens), F32),
         vm((nd, tokens, own_cols), BF16),
         vm((3 * topk, tokens), F32), vm((nd, 3 * topk, tokens), F32),
         vm((nz, tokens), F32), vm((nd, nz, tokens), F32),
         vm((nd, experts, tokens), F32), vm((nd, experts, tokens), F32),
-        vm((nd, own_rows, slots), BF16), vm((nd, own_rows, slots), BF16),
+        vm((nd, own_rows, slots), BF16),
         vm((nz, own_exp, own_cols), BF16), vm((nz, own_exp, own_cols), BF16),
-        dma((7,)), dma((9,)), dma((9,)), dma((nz,)), dma((nz, nz)), dma((nz,)),
+        dma((7,)), dma((9,)), dma((9,)), dma((nz,)), dma((len(SLOT),)), dma((nz,)),
     ]
     vm_spec = pl.BlockSpec(memory_space=pltpu.VMEM)
     held = 2 * tokens * width + 4 * own_exp * own_cols + 4 * own_rows * width + 2 * slots * hidden_units
-    token_grad, router_grad, down_grad, hidden_grad = pl.pallas_call(
+    held = held + 2 * nd * slots * width + 2 * nd * own_rows * 128
+    results = pl.pallas_call(
         functools.partial(layer_kernel, nd, nz, cap),
         out_shape=(
             pltpu.VMEM((tokens, width), BF16),
             pltpu.VMEM((own_exp, own_cols), F32),
             pltpu.VMEM((own_rows, width), F32),
             pltpu.VMEM((slots, hidden_units), BF16),
+            pltpu.VMEM((nd, nz, cap, width), BF16),
+            pltpu.VMEM((nd, own_rows, slots), BF16),
         ),
         in_specs=[pl.BlockSpec(memory_space=pltpu.HBM)] * 7,
-        out_specs=(vm_spec,) * 4,
+        out_specs=(vm_spec,) * 6,
         scratch_shapes=scratch,
         compiler_params=pltpu.CompilerParams(
             collective_id=0, has_side_effects=True, vmem_limit_bytes=VMEM_BYTES - held
@@ -442,8 +511,7 @@
         tokens_in, out_grad, expert_ids.T, rest_scores.T, router_weight,
         down_weight[0], saved_hidden.reshape(slots, hidden_units),
     )
-    results = (token_grad, router_grad, down_grad, hidden_grad)
-    token_grad, router_grad, down_grad, hidden_grad = hand_out(results)
+    token_grad, router_grad, down_grad, hidden_grad = hand_out(nd, results)
     return token_grad, router_grad.T, down_grad[None], hidden_grad.reshape(saved_hidden.shape)
 
 

time: 29.7 us -> 27.7 us (0.933); the launches traced: 29.2 us -> 27.5 us
  Pallas kernels: 28.5 us -> 26.9 us
    pallas_call x1, Pallas kernels: 27.4 us -> 25.7 us  [fused(): pl.pallas_call(functools.partial(layer_kernel, nd, nz, cap), out_shape=(p...]
where the time goes in v2:
time: 27.7 us; the launch traced here: 27.5 us
  Pallas kernels  26.9 us (97%)
  between operations  0.64 us (2%)
    pallas_call x1, Pallas kernels, fused(): pl.pallas_call(functools.partial(layer_kernel, nd, nz, cap), out_shape=(p...  25.7 us
    pallas_call x1, Pallas kernels, hand_out(): pl.pallas_call(functools.partial(out_kernel, nd), out_shape=tuple((jax.Sh...  1.22 us

profile of v2, /device:TPU:0, one launch (start us, length us, event | category | flops | bytes accessed | tf_op | source)
XLA Modules:
  0.0 27.5 jit_solution(6254843871601747846)
XLA Ops:
  0.6 25.7 %shard_map.102 = (bf16[128,2048]{1,0:T(8,128)(2,1)S(1)}, f32[32,256]{1,0:T(8,128)S(1)}, f32[96,2048]{1,0:T(8,128)S(1)}, bf16[64,768]{1,0:T(8,128)(2,1)S(1)}, bf1...) custom-call(bf16[128,2048]{1,0:T(8,128)(2,1)} %tok_h.1, bf16[128,2048]{1,0:T(8,128)(2,1)} %grad_h.1, ...), custom_call_target="tpu_custom_call" | custom-call | tf_op jit(solution)/shard_map/pallas_call | solution.py:494
  26.3 1.2 %shard_map.103 = (bf16[128,2048]{1,0:T(8,128)(2,1)}, f32[32,256]{1,0:T(8,128)}, f32[96,2048]{1,0:T(8,128)}, bf16[64,768]{1,0:T(8,128)(2,1)}) custom-call(bf16[128,2048]{1,0:T(8,128)(2,1)S(1)} %get-tuple-element.14.token, f32[32,256]{1,0:T(8,128)S(1)} %get-tuple-element.15.router, f32[96,2048]{1,0:T(8,128)S(1)} %get-tuple-element.16.down, ...), custom_call_target="tpu_custom_call" | custom-call | tf_op jit(solution)/shard_map/pallas_call | solution.py:442
